TPU v7x, 32 devices: a whole 2x2x4 slice. The times are simulated.
32 devices in a mesh: col: 8 (over y, x, core), cuts: 4 (over z).
Axes of the slice: x: 2, y: 2, z: 4, core: 2. Of those that a mesh axis runs over, the one named last changes fastest.
Arguments:
- layout: int32 [16, 8], P(None, 'col'), may hold values from 0 to 15
- assign: int32 [16, 8], P('cuts', 'col'), may hold values from 0 to 3
- edge: bfloat16 [16, 64, 128], replicated, may hold values from -3 to 3
- gate_left: bfloat16 [8, 16, 64, 128], P('col'), may hold values from -1.5 to 1.5
- gate_right: bfloat16 [8, 16, 64, 128], P('col'), may hold values from -1.5 to 1.5
- phase_angle: float32 [4, 64], replicated, may hold values from -3.140625 to 3.140625
- close: float32 [16, 64, 128], replicated, may hold values from -6 to 6
Outputs:
- slice_amplitude: float32 [16, 2], P('cuts')
- slice_log: float32 [16], P('cuts')
- total_amp: float32 [2], replicated
- top_log: float32 [], replicated
All inputs are finite; a program needn't handle non-finite values. Where the computation divides by a largest or mean magnitude, that divisor is 1e-20 or more.
Results may differ from a plain program's by a relative error of at most 0.0003.
Values sent between devices are 32-bit elements; how exact they have to be, the bound alone decides.
A program may use at most 64 MiB of HBM per device.

v0:
```python
import math

import jax
import jax.numpy as jnp
from jax import lax
from jax.sharding import PartitionSpec as P

BLK = 1


def from_behind(value, axis, by):
    length = lax.axis_size(axis)
    pairs = [(i, i + by) for i in range(length) if 0 <= i + by < length]
    return lax.ppermute(value, axis, pairs)


def one_hot(values, count, dtype):
    return (values[..., None] == jnp.arange(count, dtype=jnp.int32)).astype(dtype)


def sweep_column(board, left_sel, right_sel, cosine, sine):
    width = board.shape[-2]
    below = jnp.concatenate([board[:, 1:], jnp.zeros_like(board[:, :1])], axis=1)
    mixed = board + 0.5 * below
    left_four = left_sel.reshape(left_sel.shape[0], width, 2, width)
    stacked = jnp.einsum("rpka,srab->srkpb", left_four, mixed, precision=lax.Precision.HIGHEST)
    former = stacked[:, :, 0]
    latter = stacked[:, :, 1]
    real_part = former[..., :width] - latter[..., width:]
    imag_part = former[..., width:] + latter[..., :width]
    from_real = jnp.einsum("srab,rbq->sraq", real_part, right_sel, precision=lax.Precision.HIGHEST)
    from_imag = jnp.einsum("srab,rbq->sraq", imag_part, right_sel, precision=lax.Precision.HIGHEST)
    out_real = from_real[..., :width] - from_imag[..., width:]
    out_imag = from_real[..., width:] + from_imag[..., :width]
    cos_rows = cosine[:, None, None, :]
    sin_rows = sine[:, None, None, :]
    turned_real = out_real * cos_rows - out_imag * sin_rows
    turned_imag = out_real * sin_rows + out_imag * cos_rows
    peaks = jnp.maximum(
        jnp.max(jnp.abs(turned_real), axis=(1, 2, 3)), jnp.max(jnp.abs(turned_imag), axis=(1, 2, 3))
    )
    peaks = jnp.maximum(peaks, 1.0)
    board = jnp.concatenate([turned_real, turned_imag], -1) / peaks[:, None, None, None]
    return (board, jnp.log(peaks))


def amplitude(board, close):
    width = close.shape[-1] // 2
    b_real = board[..., :width]
    b_imag = board[..., width:]
    c_real = close[..., :width]
    c_imag = close[..., width:]
    factor = 1.0 / math.sqrt(close.shape[0] * width * width)
    amp_real = jnp.sum(b_real * c_real - b_imag * c_imag, axis=(1, 2, 3)) * factor
    amp_imag = jnp.sum(b_real * c_imag + b_imag * c_real, axis=(1, 2, 3)) * factor
    return jnp.stack([amp_real, amp_imag], -1)


def body(layout, assign, edge, gate_left, gate_right, phase_angle, close):
    sections = lax.axis_size("col")
    place = lax.axis_index("col")
    kinds = gate_left.shape[1]
    values = phase_angle.shape[0]
    per_device = assign.shape[0]
    group = BLK
    groups = per_device // group
    row_hot = one_hot(layout.T, kinds, jnp.bfloat16)
    left_all = jnp.einsum("crg,cgpq->crpq", row_hot, gate_left, preferred_element_type=jnp.float32)
    right_all = jnp.einsum(
        "crg,cgpq->crpq", row_hot, gate_right, preferred_element_type=jnp.float32
    )
    cos_table = jnp.cos(phase_angle)
    sin_table = jnp.sin(phase_angle)
    start_board = edge.astype(jnp.float32)[None]

    def run_columns(board, assign_group):
        value_hot = one_hot(assign_group, values, jnp.float32)
        cos_sel = jnp.einsum("scq,qb->scb", value_hot, cos_table, precision=lax.Precision.HIGHEST)
        sin_sel = jnp.einsum("scq,qb->scb", value_hot, sin_table, precision=lax.Precision.HIGHEST)
        board, scales = sweep_column(board, left_all[0], right_all[0], cos_sel[:, 0], sin_sel[:, 0])
        return (board, scales)

    def section(step, carry):
        held_board, amps, logs = carry
        index = step - place
        valid = jnp.logical_and(index >= 0, index < groups)
        safe = jnp.clip(index, 0, groups - 1)
        first = place == 0
        board = jnp.where(first, start_board, held_board)
        assign_group = lax.dynamic_slice_in_dim(assign, safe * group, group, 0)
        board, scales = lax.cond(
            valid,
            lambda: run_columns(board, assign_group),
            lambda: (board, jnp.zeros((group,), jnp.float32)),
        )
        keep = jnp.logical_and(valid, place == sections - 1)
        amps = jnp.where(
            keep,
            lax.dynamic_update_slice_in_dim(amps, amplitude(board, close), safe * group, 0),
            amps,
        )
        logs = jnp.where(
            valid, lax.dynamic_update_slice_in_dim(logs, scales, safe * group, 0), logs
        )
        held_board = from_behind(board, "col", 1)
        return (held_board, amps, logs)

    initial = (
        start_board,
        jnp.zeros((per_device, 2), jnp.float32),
        jnp.zeros((per_device,), jnp.float32),
    )
    unused_board, amps, logs = lax.fori_loop(0, sections + groups - 1, section, initial)
    amps, logs = lax.psum((amps, logs), "col")
    local_top = jnp.max(logs)
    top_log = lax.pmax(local_top, "cuts")
    partial_sum = jnp.sum(amps * jnp.exp(logs - top_log)[:, None], axis=0)
    total_amp = lax.psum(partial_sum, "cuts")
    return (amps, logs, total_amp, top_log)


def solution(mesh):
    in_specs = (
        P(None, "col"),
        P("cuts", "col"),
        P(),
        P("col", None, None, None),
        P("col", None, None, None),
        P(),
        P(),
    )
    out_specs = (P("cuts", None), P("cuts"), P(), P())
    return jax.shard_map(body, mesh=mesh, in_specs=in_specs, out_specs=out_specs, check_vma=False)
```

profile of v0, /device:TPU:0, one launch (start us, length us, event | category | flops | bytes accessed | tf_op | source)
XLA Modules:
  0.0 233.8 jit_solution(1438739594680837306)
XLA Ops:
  0.7 0.9 copy-done
  2.5 1.0 copy.15
  4.0 0.8 copy-done.4
  6.2 168.6 %while.18 = (s32[]{:T(128)}, f32[1,16,64,128]{3,2,1,0:T(8,128)S(1)}, f32[4,2]{0,1:T(2,128)S(1)}, f32[4]{0:T(128)S(1)}, s32[]{:T(128)}, /*index=5*/pred[]{:T(512)...) while((s32[]{:T(128)}, ...), condition=%wide.region_7.8_spmd, body=%wide.region_0.7_spmd.sunk | while | flops 404756480 | bytes 22449744 | solution.py:113
  7.0 8.9 %conditional.2 = (f32[1,16,64,128]{3,2,1,0:T(8,128)S(1)}, f32[1]{0:T(128)}) conditional(s32[]{:T(128)} %convert_element_type.12, f32[1,16,64,128]{3,2,1,0:T(8,128)S(1)} %broadcast_select_fusion.2, (f32[1,16,64,128]{3,2,1,0:T(8,128)S(1)}, f32[1,16,64,128]{3,2,1,0:T(8,128)}, f32[1,16,64,128]{3,2,1,0:T(8,128)S(1)}, s32[4,1]{0,1:T(1,128)S(1)}, s32[]{:T(128)}, ...), branch_computations={%region_1.1_spmd, %region_2.4_spmd} | conditional | flops 404101120 | bytes 13536336 | solution.py:91
  7.1 1.7 squeeze.14
  8.7 1.0 convolution_bitcast_fusion
  12.7 0.8 convolution_bitcast_fusion.4
  13.5 1.0 abs_reduce_fusion.1
  16.0 1.3 collective-permute-start
  17.3 1.0 fusion.39
  20.6 8.9 %conditional.2 = (f32[1,16,64,128]{3,2,1,0:T(8,128)S(1)}, f32[1]{0:T(128)}) conditional(s32[]{:T(128)} %convert_element_type.12, f32[1,16,64,128]{3,2,1,0:T(8,128)S(1)} %broadcast_select_fusion.2, (f32[1,16,64,128]{3,2,1,0:T(8,128)S(1)}, f32[1,16,64,128]{3,2,1,0:T(8,128)}, f32[1,16,64,128]{3,2,1,0:T(8,128)S(1)}, s32[4,1]{0,1:T(1,128)S(1)}, s32[]{:T(128)}, ...), branch_computations={%region_1.1_spmd, %region_2.4_spmd} | conditional | flops 404101120 | bytes 13536336 | solution.py:91
  20.6 1.7 squeeze.14
  22.3 1.0 convolution_bitcast_fusion
  26.3 0.8 convolution_bitcast_fusion.4
  27.1 1.0 abs_reduce_fusion.1
  29.5 1.3 collective-permute-start
  30.9 1.0 fusion.39
  34.2 8.9 %conditional.2 = (f32[1,16,64,128]{3,2,1,0:T(8,128)S(1)}, f32[1]{0:T(128)}) conditional(s32[]{:T(128)} %convert_element_type.12, f32[1,16,64,128]{3,2,1,0:T(8,128)S(1)} %broadcast_select_fusion.2, (f32[1,16,64,128]{3,2,1,0:T(8,128)S(1)}, f32[1,16,64,128]{3,2,1,0:T(8,128)}, f32[1,16,64,128]{3,2,1,0:T(8,128)S(1)}, s32[4,1]{0,1:T(1,128)S(1)}, s32[]{:T(128)}, ...), branch_computations={%region_1.1_spmd, %region_2.4_spmd} | conditional | flops 404101120 | bytes 13536336 | solution.py:91
  34.3 1.7 squeeze.14
  35.9 1.0 convolution_bitcast_fusion
  39.9 0.8 convolution_bitcast_fusion.4
  40.7 1.0 abs_reduce_fusion.1
  43.2 5.5 %collective-permute-start = (f32[1,16,64,128]{3,2,1,0:T(8,128)S(1)}, f32[1,16,64,128]{3,2,1,0:T(8,128)S(1)}, u32[]{:S(2)}, u32[]{:S(2)}) collective-permute-start(f32[1,16,64,128]{3,2,1,0:T(8,128)S(1)} %get-tuple-element.447), channel_id=1, source_target_pairs={{0,4},{4,8},{8,12},{12,16},{16,20},{20,24},{24,28},{1,5},{5,9},{9,... | collective-permute-start | bytes 1572872 | tf_op jit(solution)/shard_map/while/body/eval_jaxpr/ppermute | solution.py:14
  48.7 1.0 fusion.39
  52.0 8.9 %conditional.2 = (f32[1,16,64,128]{3,2,1,0:T(8,128)S(1)}, f32[1]{0:T(128)}) conditional(s32[]{:T(128)} %convert_element_type.12, f32[1,16,64,128]{3,2,1,0:T(8,128)S(1)} %broadcast_select_fusion.2, (f32[1,16,64,128]{3,2,1,0:T(8,128)S(1)}, f32[1,16,64,128]{3,2,1,0:T(8,128)}, f32[1,16,64,128]{3,2,1,0:T(8,128)S(1)}, s32[4,1]{0,1:T(1,128)S(1)}, s32[]{:T(128)}, ...), branch_computations={%region_1.1_spmd, %region_2.4_spmd} | conditional | flops 404101120 | bytes 13536336 | solution.py:91
  52.1 1.7 squeeze.14
  53.7 1.0 convolution_bitcast_fusion
  58.5 1.0 abs_reduce_fusion.1
  61.0 7.9 %collective-permute-start = (f32[1,16,64,128]{3,2,1,0:T(8,128)S(1)}, f32[1,16,64,128]{3,2,1,0:T(8,128)S(1)}, u32[]{:S(2)}, u32[]{:S(2)}) collective-permute-start(f32[1,16,64,128]{3,2,1,0:T(8,128)S(1)} %get-tuple-element.447), channel_id=1, source_target_pairs={{0,4},{4,8},{8,12},{12,16},{16,20},{20,24},{24,28},{1,5},{5,9},{9,... | collective-permute-start | bytes 1572872 | tf_op jit(solution)/shard_map/while/body/eval_jaxpr/ppermute | solution.py:14
  68.9 1.0 fusion.39
  72.3 16.9 %collective-permute-start = (f32[1,16,64,128]{3,2,1,0:T(8,128)S(1)}, f32[1,16,64,128]{3,2,1,0:T(8,128)S(1)}, u32[]{:S(2)}, u32[]{:S(2)}) collective-permute-start(f32[1,16,64,128]{3,2,1,0:T(8,128)S(1)} %get-tuple-element.447), channel_id=1, source_target_pairs={{0,4},{4,8},{8,12},{12,16},{16,20},{20,24},{24,28},{1,5},{5,9},{9,... | collective-permute-start | bytes 1572872 | tf_op jit(solution)/shard_map/while/body/eval_jaxpr/ppermute | solution.py:14
  89.2 1.0 fusion.39
  92.5 7.9 %collective-permute-start = (f32[1,16,64,128]{3,2,1,0:T(8,128)S(1)}, f32[1,16,64,128]{3,2,1,0:T(8,128)S(1)}, u32[]{:S(2)}, u32[]{:S(2)}) collective-permute-start(f32[1,16,64,128]{3,2,1,0:T(8,128)S(1)} %get-tuple-element.447), channel_id=1, source_target_pairs={{0,4},{4,8},{8,12},{12,16},{16,20},{20,24},{24,28},{1,5},{5,9},{9,... | collective-permute-start | bytes 1572872 | tf_op jit(solution)/shard_map/while/body/eval_jaxpr/ppermute | solution.py:14
  100.5 1.0 fusion.39
  103.8 16.9 %collective-permute-start = (f32[1,16,64,128]{3,2,1,0:T(8,128)S(1)}, f32[1,16,64,128]{3,2,1,0:T(8,128)S(1)}, u32[]{:S(2)}, u32[]{:S(2)}) collective-permute-start(f32[1,16,64,128]{3,2,1,0:T(8,128)S(1)} %get-tuple-element.447), channel_id=1, source_target_pairs={{0,4},{4,8},{8,12},{12,16},{16,20},{20,24},{24,28},{1,5},{5,9},{9,... | collective-permute-start | bytes 1572872 | tf_op jit(solution)/shard_map/while/body/eval_jaxpr/ppermute | solution.py:14
  120.7 1.0 fusion.39
  124.1 7.9 %collective-permute-start = (f32[1,16,64,128]{3,2,1,0:T(8,128)S(1)}, f32[1,16,64,128]{3,2,1,0:T(8,128)S(1)}, u32[]{:S(2)}, u32[]{:S(2)}) collective-permute-start(f32[1,16,64,128]{3,2,1,0:T(8,128)S(1)} %get-tuple-element.447), channel_id=1, source_target_pairs={{0,4},{4,8},{8,12},{12,16},{16,20},{20,24},{24,28},{1,5},{5,9},{9,... | collective-permute-start | bytes 1572872 | tf_op jit(solution)/shard_map/while/body/eval_jaxpr/ppermute | solution.py:14
  132.0 1.0 fusion.39
  135.4 7.9 %collective-permute-start = (f32[1,16,64,128]{3,2,1,0:T(8,128)S(1)}, f32[1,16,64,128]{3,2,1,0:T(8,128)S(1)}, u32[]{:S(2)}, u32[]{:S(2)}) collective-permute-start(f32[1,16,64,128]{3,2,1,0:T(8,128)S(1)} %get-tuple-element.447), channel_id=1, source_target_pairs={{0,4},{4,8},{8,12},{12,16},{16,20},{20,24},{24,28},{1,5},{5,9},{9,... | collective-permute-start | bytes 1572872 | tf_op jit(solution)/shard_map/while/body/eval_jaxpr/ppermute | solution.py:14
  143.3 1.0 fusion.39
  146.7 7.9 %collective-permute-start = (f32[1,16,64,128]{3,2,1,0:T(8,128)S(1)}, f32[1,16,64,128]{3,2,1,0:T(8,128)S(1)}, u32[]{:S(2)}, u32[]{:S(2)}) collective-permute-start(f32[1,16,64,128]{3,2,1,0:T(8,128)S(1)} %get-tuple-element.447), channel_id=1, source_target_pairs={{0,4},{4,8},{8,12},{12,16},{16,20},{20,24},{24,28},{1,5},{5,9},{9,... | collective-permute-start | bytes 1572872 | tf_op jit(solution)/shard_map/while/body/eval_jaxpr/ppermute | solution.py:14
  154.7 1.0 fusion.39
  158.0 14.2 %collective-permute-start = (f32[1,16,64,128]{3,2,1,0:T(8,128)S(1)}, f32[1,16,64,128]{3,2,1,0:T(8,128)S(1)}, u32[]{:S(2)}, u32[]{:S(2)}) collective-permute-start(f32[1,16,64,128]{3,2,1,0:T(8,128)S(1)} %get-tuple-element.447), channel_id=1, source_target_pairs={{0,4},{4,8},{8,12},{12,16},{16,20},{20,24},{24,28},{1,5},{5,9},{9,... | collective-permute-start | bytes 1572872 | tf_op jit(solution)/shard_map/while/body/eval_jaxpr/ppermute | solution.py:14
  172.3 1.0 fusion.39
  174.8 34.6 %all-reduce.1 = (f32[4,2]{0,1:T(2,128)S(1)}, f32[4]{0:T(128)S(1)}) all-reduce(f32[4,2]{0,1:T(2,128)S(1)} %get-tuple-element.300, f32[4]{0:T(128)S(1)} %get-tuple-element.301), channel_id=1, replica_groups=mesh['col'=8,'cuts'=4] {'col'}, use_global_device_ids=true, to_apply=%region_8.9 | all-reduce | flops 12 | bytes 96 | tf_op jit(solution)/shard_map/psum | solution.py:114
  210.1 14.0 %pmax.7 = f32[]{:T(128)} all-reduce(f32[]{:T(128)} %reduce_max.27), channel_id=1, replica_groups=mesh['col'=8,'cuts'=4] {'cuts'}, use_global_device_ids=true, to_apply=%region_11.12 | all-reduce | flops 1 | bytes 8 | tf_op jit(solution)/shard_map/pmax | solution.py:116
  224.9 8.9 %psum.23 = f32[2]{0:T(128)} all-reduce(f32[2]{0:T(128)S(1)} %multiply_reduce_fusion), channel_id=1, replica_groups=mesh['col'=8,'cuts'=4] {'cuts'}, use_global_device_ids=true, to_apply=%region_13.14 | all-reduce | flops 2 | bytes 16 | tf_op jit(solution)/shard_map/psum | solution.py:118
  (162 shorter events, 29.9 us)
Async XLA Ops:
  0.6 1.0 copy-start
  1.6 0.7 copy-start.7
  2.5 1.0 copy-start.5
  3.8 1.0 copy-start.4
  4.8 0.7 copy-start.6
  4.8 1.0 copy-start.1
  5.5 0.7 copy-start.9
  6.2 0.8 copy-start.2
  16.0 3.8 %collective-permute-start = (f32[1,16,64,128]{3,2,1,0:T(8,128)S(1)}, f32[1,16,64,128]{3,2,1,0:T(8,128)S(1)}, u32[]{:S(2)}, u32[]{:S(2)}) collective-permute-start(f32[1,16,64,128]{3,2,1,0:T(8,128)S(1)} %get-tuple-element.447), channel_id=1, source_target_pairs={{0,4},{4,8},{8,12},{12,16},{16,20},{20,24},{24,28},{1,5},{5,9},{9,... | collective-permute-start | bytes 1572872 | tf_op jit(solution)/shard_map/while/body/eval_jaxpr/ppermute | solution.py:14
  17.3 2.5 %copy-start.3 = (f32[1,16,64,128]{3,2,1,0:T(8,128)S(1)}, f32[1,16,64,128]{3,2,1,0:T(8,128)}, u32[]{:S(2)}) copy-start(f32[1,16,64,128]{3,2,1,0:T(8,128)} %copy-done.2) | copy-start | bytes 1572868 | tf_op jit(solution)/shard_map/while
  19.8 0.8 copy-start.2
  29.5 3.9 %collective-permute-start = (f32[1,16,64,128]{3,2,1,0:T(8,128)S(1)}, f32[1,16,64,128]{3,2,1,0:T(8,128)S(1)}, u32[]{:S(2)}, u32[]{:S(2)}) collective-permute-start(f32[1,16,64,128]{3,2,1,0:T(8,128)S(1)} %get-tuple-element.447), channel_id=1, source_target_pairs={{0,4},{4,8},{8,12},{12,16},{16,20},{20,24},{24,28},{1,5},{5,9},{9,... | collective-permute-start | bytes 1572872 | tf_op jit(solution)/shard_map/while/body/eval_jaxpr/ppermute | solution.py:14
  30.9 2.5 %copy-start.3 = (f32[1,16,64,128]{3,2,1,0:T(8,128)S(1)}, f32[1,16,64,128]{3,2,1,0:T(8,128)}, u32[]{:S(2)}) copy-start(f32[1,16,64,128]{3,2,1,0:T(8,128)} %copy-done.2) | copy-start | bytes 1572868 | tf_op jit(solution)/shard_map/while
  33.4 0.8 copy-start.2
  43.2 8.0 %collective-permute-start = (f32[1,16,64,128]{3,2,1,0:T(8,128)S(1)}, f32[1,16,64,128]{3,2,1,0:T(8,128)S(1)}, u32[]{:S(2)}, u32[]{:S(2)}) collective-permute-start(f32[1,16,64,128]{3,2,1,0:T(8,128)S(1)} %get-tuple-element.447), channel_id=1, source_target_pairs={{0,4},{4,8},{8,12},{12,16},{16,20},{20,24},{24,28},{1,5},{5,9},{9,... | collective-permute-start | bytes 1572872 | tf_op jit(solution)/shard_map/while/body/eval_jaxpr/ppermute | solution.py:14
  48.7 2.5 %copy-start.3 = (f32[1,16,64,128]{3,2,1,0:T(8,128)S(1)}, f32[1,16,64,128]{3,2,1,0:T(8,128)}, u32[]{:S(2)}) copy-start(f32[1,16,64,128]{3,2,1,0:T(8,128)} %copy-done.2) | copy-start | bytes 1572868 | tf_op jit(solution)/shard_map/while
  51.2 0.8 copy-start.2
  61.0 10.5 %collective-permute-start = (f32[1,16,64,128]{3,2,1,0:T(8,128)S(1)}, f32[1,16,64,128]{3,2,1,0:T(8,128)S(1)}, u32[]{:S(2)}, u32[]{:S(2)}) collective-permute-start(f32[1,16,64,128]{3,2,1,0:T(8,128)S(1)} %get-tuple-element.447), channel_id=1, source_target_pairs={{0,4},{4,8},{8,12},{12,16},{16,20},{20,24},{24,28},{1,5},{5,9},{9,... | collective-permute-start | bytes 1572872 | tf_op jit(solution)/shard_map/while/body/eval_jaxpr/ppermute | solution.py:14
  68.9 2.5 %copy-start.3 = (f32[1,16,64,128]{3,2,1,0:T(8,128)S(1)}, f32[1,16,64,128]{3,2,1,0:T(8,128)}, u32[]{:S(2)}) copy-start(f32[1,16,64,128]{3,2,1,0:T(8,128)} %copy-done.2) | copy-start | bytes 1572868 | tf_op jit(solution)/shard_map/while
  71.5 0.8 copy-start.2
  72.3 19.4 %collective-permute-start = (f32[1,16,64,128]{3,2,1,0:T(8,128)S(1)}, f32[1,16,64,128]{3,2,1,0:T(8,128)S(1)}, u32[]{:S(2)}, u32[]{:S(2)}) collective-permute-start(f32[1,16,64,128]{3,2,1,0:T(8,128)S(1)} %get-tuple-element.447), channel_id=1, source_target_pairs={{0,4},{4,8},{8,12},{12,16},{16,20},{20,24},{24,28},{1,5},{5,9},{9,... | collective-permute-start | bytes 1572872 | tf_op jit(solution)/shard_map/while/body/eval_jaxpr/ppermute | solution.py:14
  89.2 2.5 %copy-start.3 = (f32[1,16,64,128]{3,2,1,0:T(8,128)S(1)}, f32[1,16,64,128]{3,2,1,0:T(8,128)}, u32[]{:S(2)}) copy-start(f32[1,16,64,128]{3,2,1,0:T(8,128)} %copy-done.2) | copy-start | bytes 1572868 | tf_op jit(solution)/shard_map/while
  91.7 0.8 copy-start.2
  92.5 10.5 %collective-permute-start = (f32[1,16,64,128]{3,2,1,0:T(8,128)S(1)}, f32[1,16,64,128]{3,2,1,0:T(8,128)S(1)}, u32[]{:S(2)}, u32[]{:S(2)}) collective-permute-start(f32[1,16,64,128]{3,2,1,0:T(8,128)S(1)} %get-tuple-element.447), channel_id=1, source_target_pairs={{0,4},{4,8},{8,12},{12,16},{16,20},{20,24},{24,28},{1,5},{5,9},{9,... | collective-permute-start | bytes 1572872 | tf_op jit(solution)/shard_map/while/body/eval_jaxpr/ppermute | solution.py:14
  100.5 2.5 %copy-start.3 = (f32[1,16,64,128]{3,2,1,0:T(8,128)S(1)}, f32[1,16,64,128]{3,2,1,0:T(8,128)}, u32[]{:S(2)}) copy-start(f32[1,16,64,128]{3,2,1,0:T(8,128)} %copy-done.2) | copy-start | bytes 1572868 | tf_op jit(solution)/shard_map/while
  103.0 0.8 copy-start.2
  103.8 19.4 %collective-permute-start = (f32[1,16,64,128]{3,2,1,0:T(8,128)S(1)}, f32[1,16,64,128]{3,2,1,0:T(8,128)S(1)}, u32[]{:S(2)}, u32[]{:S(2)}) collective-permute-start(f32[1,16,64,128]{3,2,1,0:T(8,128)S(1)} %get-tuple-element.447), channel_id=1, source_target_pairs={{0,4},{4,8},{8,12},{12,16},{16,20},{20,24},{24,28},{1,5},{5,9},{9,... | collective-permute-start | bytes 1572872 | tf_op jit(solution)/shard_map/while/body/eval_jaxpr/ppermute | solution.py:14
  120.7 2.5 %copy-start.3 = (f32[1,16,64,128]{3,2,1,0:T(8,128)S(1)}, f32[1,16,64,128]{3,2,1,0:T(8,128)}, u32[]{:S(2)}) copy-start(f32[1,16,64,128]{3,2,1,0:T(8,128)} %copy-done.2) | copy-start | bytes 1572868 | tf_op jit(solution)/shard_map/while
  123.3 0.8 copy-start.2
  124.1 10.5 %collective-permute-start = (f32[1,16,64,128]{3,2,1,0:T(8,128)S(1)}, f32[1,16,64,128]{3,2,1,0:T(8,128)S(1)}, u32[]{:S(2)}, u32[]{:S(2)}) collective-permute-start(f32[1,16,64,128]{3,2,1,0:T(8,128)S(1)} %get-tuple-element.447), channel_id=1, source_target_pairs={{0,4},{4,8},{8,12},{12,16},{16,20},{20,24},{24,28},{1,5},{5,9},{9,... | collective-permute-start | bytes 1572872 | tf_op jit(solution)/shard_map/while/body/eval_jaxpr/ppermute | solution.py:14
  132.0 2.5 %copy-start.3 = (f32[1,16,64,128]{3,2,1,0:T(8,128)S(1)}, f32[1,16,64,128]{3,2,1,0:T(8,128)}, u32[]{:S(2)}) copy-start(f32[1,16,64,128]{3,2,1,0:T(8,128)} %copy-done.2) | copy-start | bytes 1572868 | tf_op jit(solution)/shard_map/while
  134.6 0.8 copy-start.2
  135.4 10.5 %collective-permute-start = (f32[1,16,64,128]{3,2,1,0:T(8,128)S(1)}, f32[1,16,64,128]{3,2,1,0:T(8,128)S(1)}, u32[]{:S(2)}, u32[]{:S(2)}) collective-permute-start(f32[1,16,64,128]{3,2,1,0:T(8,128)S(1)} %get-tuple-element.447), channel_id=1, source_target_pairs={{0,4},{4,8},{8,12},{12,16},{16,20},{20,24},{24,28},{1,5},{5,9},{9,... | collective-permute-start | bytes 1572872 | tf_op jit(solution)/shard_map/while/body/eval_jaxpr/ppermute | solution.py:14
  143.3 2.5 %copy-start.3 = (f32[1,16,64,128]{3,2,1,0:T(8,128)S(1)}, f32[1,16,64,128]{3,2,1,0:T(8,128)}, u32[]{:S(2)}) copy-start(f32[1,16,64,128]{3,2,1,0:T(8,128)} %copy-done.2) | copy-start | bytes 1572868 | tf_op jit(solution)/shard_map/while
  145.9 0.8 copy-start.2
  146.7 10.5 %collective-permute-start = (f32[1,16,64,128]{3,2,1,0:T(8,128)S(1)}, f32[1,16,64,128]{3,2,1,0:T(8,128)S(1)}, u32[]{:S(2)}, u32[]{:S(2)}) collective-permute-start(f32[1,16,64,128]{3,2,1,0:T(8,128)S(1)} %get-tuple-element.447), channel_id=1, source_target_pairs={{0,4},{4,8},{8,12},{12,16},{16,20},{20,24},{24,28},{1,5},{5,9},{9,... | collective-permute-start | bytes 1572872 | tf_op jit(solution)/shard_map/while/body/eval_jaxpr/ppermute | solution.py:14
  154.6 2.5 %copy-start.3 = (f32[1,16,64,128]{3,2,1,0:T(8,128)S(1)}, f32[1,16,64,128]{3,2,1,0:T(8,128)}, u32[]{:S(2)}) copy-start(f32[1,16,64,128]{3,2,1,0:T(8,128)} %copy-done.2) | copy-start | bytes 1572868 | tf_op jit(solution)/shard_map/while
  157.2 0.8 copy-start.2
  158.0 16.8 %collective-permute-start = (f32[1,16,64,128]{3,2,1,0:T(8,128)S(1)}, f32[1,16,64,128]{3,2,1,0:T(8,128)S(1)}, u32[]{:S(2)}, u32[]{:S(2)}) collective-permute-start(f32[1,16,64,128]{3,2,1,0:T(8,128)S(1)} %get-tuple-element.447), channel_id=1, source_target_pairs={{0,4},{4,8},{8,12},{12,16},{16,20},{20,24},{24,28},{1,5},{5,9},{9,... | collective-permute-start | bytes 1572872 | tf_op jit(solution)/shard_map/while/body/eval_jaxpr/ppermute | solution.py:14
  172.3 2.5 %copy-start.3 = (f32[1,16,64,128]{3,2,1,0:T(8,128)S(1)}, f32[1,16,64,128]{3,2,1,0:T(8,128)}, u32[]{:S(2)}) copy-start(f32[1,16,64,128]{3,2,1,0:T(8,128)} %copy-done.2) | copy-start | bytes 1572868 | tf_op jit(solution)/shard_map/while
  209.5 14.7 %copy-start.10 = (f32[4]{0:T(128)}, f32[4]{0:T(128)S(1)}, u32[]{:S(2)}) copy-start(f32[4]{0:T(128)S(1)} %get-tuple-element.347) | copy-start | bytes 52
  209.5 15.3 %copy-start.8 = (f32[4,2]{0,1:T(2,128)}, f32[4,2]{0,1:T(2,128)S(1)}, u32[]{:S(2)}) copy-start(f32[4,2]{0,1:T(2,128)S(1)} %get-tuple-element.346) | copy-start | bytes 100
where the time goes:
time: 235 us; the launch traced here: 234 us
  starting transfers between devices  95.8 us (41%)
  blocking collectives  57.6 us (25%)
  local copies, waits for them, and re-layouts  23.5 us (10%)
  other arithmetic  20.2 us (9%)
  loops' own time  19.3 us (8%)
  matrix products  16.6 us (7%)
    ppermute x11, starting transfers between devices, from_behind(): return lax.ppermute(value, axis, pairs)  95.8 us
    psum x1, blocking collectives, body(): amps, logs = lax.psum((amps, logs), 'col')  34.6 us
    another operation x1, loops' own time, body(): lax.fori_loop(0, sections + groups - 1, section, initial)  14 us
    pmax x1, blocking collectives, body(): top_log = lax.pmax(local_top, 'cuts')  14 us
    reduce_sum x11, other arithmetic, amplitude(): jnp.sum(b_real * c_real - b_imag * c_imag, axis=(1, 2, 3)) * factor  10.7 us
    psum x1, blocking collectives, body(): total_amp = lax.psum(partial_sum, 'cuts')  8.87 us
    while x44, local copies, waits for them, and re-layouts  7.98 us
    squeeze x4, local copies, waits for them, and re-layouts, sweep_column(): left_four = left_sel.reshape(left_sel.shape[0], width, 2, width)  6.61 us
  transfers between devices with their start and end apart: 11, of which 0 were waited for; matrix products, arithmetic and copies ran while one was open for 6% of the time, Pallas kernels for 0%

commit v1 on v0

v1 whole, which is shorter than its diff:
```python
import functools
import math

import jax
import jax.numpy as jnp
from jax import lax
from jax.experimental import pallas as pl
from jax.experimental.pallas import tpu as pltpu
from jax.sharding import PartitionSpec as P

MESH = pl.DeviceIdType.MESH
SEGMENT = 8


def split(value):
    high = value.astype(jnp.bfloat16)
    low = (value - high.astype(jnp.float32)).astype(jnp.bfloat16)
    return high, low


def swap(value, width):
    return pltpu.roll(value, width, len(value.shape) - 1)


def kernel(
    n, nz, rows,
    layout_ref, assign_ref, edge_ref, left_ref, right_ref, cos_ref, sin_ref, close_ref,
    amp_ref, log_ref, total_ref, top_ref,
    stage, stage_phase, gates, phases, board, halo, peak, xsend, xrecv, zsend, zrecv,
    gate_send, gate_recv, halo_send, halo_recv, x_send, x_recv, z_send, z_recv,
):
    me = lax.axis_index("col")
    mz = lax.axis_index("cuts")
    per_col = left_ref.shape[0]
    columns = n * per_col
    own = rows // n
    slices = assign_ref.shape[0]
    width = left_ref.shape[2]
    lanes = 2 * width
    last = me == n - 1

    barrier = pltpu.get_barrier_semaphore()
    for k in range(1, n):
        pl.semaphore_signal(
            barrier, inc=1, device_id=(lax.rem(me + k, n), mz), device_id_type=MESH
        )
    for k in range(1, nz):
        pl.semaphore_signal(
            barrier, inc=1, device_id=(me, lax.rem(mz + k, nz)), device_id_type=MESH
        )

    lane = lax.broadcasted_iota(jnp.int32, (1, lanes), 1)
    sign = jnp.where(lane < width, -1.0, 1.0).astype(jnp.float32)

    for cl in range(per_col):
        for s in range(slices):
            value = assign_ref[s, cl]
            stage_phase[cl, pl.ds(s, 1), :] = cos_ref[pl.ds(value, 1), :]
            stage_phase[cl, pl.ds(slices + s, 1), :] = sin_ref[pl.ds(value, 1), :] * sign
        for r in range(rows):
            kind = layout_ref[r, cl]
            stage[cl, 0, r] = left_ref[cl, kind].astype(jnp.float32)
            stage[cl, 1, r] = right_ref[cl, kind].astype(jnp.float32)
    for s in range(slices):
        peak[s] = jnp.ones(peak.shape[1:], jnp.float32)

    @pl.when(last)
    def _():
        halo[...] = jnp.zeros_like(halo)

    def gate_copy(cl, part, target):
        column = me * per_col + cl
        if part == 2:
            source, sink = stage_phase.at[cl], phases.at[column]
        else:
            source = stage.at[cl, part, pl.ds(target * own, own)]
            sink = gates.at[column, part]
        return pltpu.make_async_remote_copy(
            src_ref=source,
            dst_ref=sink,
            send_sem=gate_send.at[cl, part, target],
            recv_sem=gate_recv.at[column, part],
            device_id=(target, mz),
            device_id_type=MESH,
        )

    pl.semaphore_wait(barrier, n - 1 + nz - 1)
    for cl in range(per_col):
        for part in (2, 0, 1):
            for k in range(1, n):
                gate_copy(cl, part, lax.rem(me + k, n)).start()
    for cl in range(per_col):
        column = me * per_col + cl
        phases[column] = stage_phase[cl]
        for part in range(2):
            gates[column, part] = stage[cl, part, pl.ds(me * own, own)]

    def wait_gates(column, part):
        sink = phases.at[column] if part == 2 else gates.at[column, part]

        @pl.when(column // per_col != me)
        def _():
            pltpu.make_async_remote_copy(
                src_ref=sink,
                dst_ref=sink,
                send_sem=gate_send.at[0, part, 0],
                recv_sem=gate_recv.at[column, part],
                device_id=(lax.rem(me + 1, n), mz),
                device_id_type=MESH,
            ).wait_recv()

    def halo_copy(column):
        return pltpu.make_async_remote_copy(
            src_ref=board.at[column, 0],
            dst_ref=halo.at[column],
            send_sem=halo_send.at[column],
            recv_sem=halo_recv.at[column],
            device_id=(lax.rem(me + n - 1, n), mz),
            device_id_type=MESH,
        )

    def one_row(column, r, mixed, right_wait):
        left = gates[column, 0, r].astype(jnp.bfloat16)
        left = jnp.concatenate([left, left], axis=1)
        stacks = []
        for m in mixed:
            high, low = split(m)
            turned_high, turned_low = split(swap(m, width) * sign)
            stacks.append(jnp.concatenate([high, turned_high, low, turned_low], axis=0))
        middle = jnp.dot(
            left, jnp.concatenate(stacks, axis=1), preferred_element_type=jnp.float32
        )
        if right_wait:
            wait_gates(column, 1)
            wait_gates(column, 2)
        right = gates[column, 1, r]
        right = jnp.concatenate([right, swap(right, width) * sign], axis=0).astype(jnp.bfloat16)
        right = jnp.concatenate([right, right], axis=0)
        high, low = split(
            jnp.concatenate([middle[:, i * lanes:(i + 1) * lanes] for i in range(len(mixed))], axis=0)
        )
        outs = jnp.dot(
            jnp.concatenate([high, low], axis=1), right, preferred_element_type=jnp.float32
        )
        for s in range(slices):
            i = s if len(mixed) > 1 else 0
            out = outs[i * width:(i + 1) * width]
            if len(mixed) == 1 and s > 0:
                out_swapped = first_swapped
            else:
                out_swapped = swap(out, width)
                first_swapped = out_swapped
            turned = out * phases[column, pl.ds(s, 1), :] + out_swapped * phases[
                column, pl.ds(slices + s, 1), :
            ]
            board[column, r, s] = turned
            size = jnp.abs(turned).reshape(width // 8, 8, lanes)
            peak[s] = jnp.maximum(peak[s], jnp.max(size, axis=0))

    def after_row(column, r):
        if r == 0:
            @pl.when(me > 0)
            def _():
                halo_copy(column).start()

    wait_gates(0, 0)
    for r in range(own):
        row = me * own + r
        here = edge_ref[row].astype(jnp.float32)
        if r + 1 < own:
            below = 0.5 * edge_ref[row + 1].astype(jnp.float32)
        else:
            weight = jnp.where(last, 0.0, 0.5).astype(jnp.float32)
            below = weight * edge_ref[jnp.minimum(row + 1, rows - 1)].astype(jnp.float32)
        one_row(0, r, [here + below], r == 0)
        if columns > 1:
            after_row(0, r)

    def column_step(column, scale, send):
        wait_gates(column, 0)
        for r in range(own):
            if r + 1 == own:
                @pl.when(jnp.logical_not(last))
                def _():
                    halo_copy(column - 1).wait_recv()
            mixed = []
            for s in range(slices):
                below = board[column - 1, r + 1, s] if r + 1 < own else halo[column - 1, s]
                m = board[column - 1, r, s] + 0.5 * below
                mixed.append(m if scale is None else m * scale[s])
            one_row(column, r, mixed, r == 0)
            if send:
                after_row(column, r)

    def exchange(slot, count, index, axis_copy, sender, receiver):
        def copy(target):
            return axis_copy(slot, target)

        receiver[slot, index] = sender[slot]
        for k in range(1, count):
            copy(lax.rem(index + k, count)).start()
        for k in range(1, count):
            copy(lax.rem(index + k, count)).wait_send()

    def x_copy(slot, target):
        return pltpu.make_async_remote_copy(
            src_ref=xsend.at[slot],
            dst_ref=xrecv.at[slot, me],
            send_sem=x_send.at[slot, target],
            recv_sem=x_recv.at[slot, me],
            device_id=(target, mz),
            device_id_type=MESH,
        )

    def x_wait(slot):
        for k in range(1, n):
            source = lax.rem(me + k, n)
            pltpu.make_async_remote_copy(
                src_ref=xsend.at[slot],
                dst_ref=xrecv.at[slot, source],
                send_sem=x_send.at[slot, source],
                recv_sem=x_recv.at[slot, source],
                device_id=(source, mz),
                device_id_type=MESH,
            ).wait_recv()

    def z_copy(target):
        return pltpu.make_async_remote_copy(
            src_ref=zsend,
            dst_ref=zrecv.at[mz],
            send_sem=z_send.at[target],
            recv_sem=z_recv.at[mz],
            device_id=(me, target),
            device_id_type=MESH,
        )

    def local_peaks():
        return [
            jnp.max(jnp.max(peak[s], axis=0, keepdims=True), axis=1, keepdims=True)
            for s in range(slices)
        ]

    logs = [jnp.zeros((1, 1), jnp.float32)] * slices
    scale = None
    begin, slot = 1, 0
    while True:
        stop = min(columns, (begin // SEGMENT + 1) * SEGMENT)
        if scale is not None:
            column_step(begin, scale, begin + 1 < columns)
            begin += 1
        full = min(stop, columns - 1)

        def loop_step(column, carry):
            column_step(column, None, True)
            return carry

        if full > begin:
            lax.fori_loop(begin, full, loop_step, 0)
        if stop == columns:
            if columns - 1 >= begin:
                column_step(columns - 1, None, False)
            break
        for s, m in enumerate(local_peaks()):
            xsend[slot, pl.ds(s, 1), :] = jnp.broadcast_to(m, (1, lanes))
        exchange(slot, n, me, x_copy, xsend, xrecv)
        x_wait(slot)
        scale = []
        for s in range(slices):
            m = xrecv[slot, 0, pl.ds(s, 1), :]
            for d in range(1, n):
                m = jnp.maximum(m, xrecv[slot, d, pl.ds(s, 1), :])
            logs[s] = logs[s] + jnp.log(m[:, :1])
            scale.append(1.0 / m)
            peak[s] = jnp.ones(peak.shape[1:], jnp.float32)
        begin, slot = stop, slot + 1

    factor = 1.0 / math.sqrt(rows * width * width)
    mine = local_peaks()
    for s in range(slices):
        real = jnp.zeros((8, lanes), jnp.float32)
        imag = jnp.zeros((8, lanes), jnp.float32)
        inverse = 1.0 / mine[s]
        for r in range(own):
            close = close_ref[me * own + r]
            value = board[columns - 1, r, s] * inverse
            real = real + jnp.sum((value * close).reshape(width // 8, 8, lanes), axis=0)
            imag = imag + jnp.sum((value * swap(close, width)).reshape(width // 8, 8, lanes), axis=0)
        xsend[slot, pl.ds(s, 1), :] = jnp.sum(real, axis=0, keepdims=True) * (-sign)
        xsend[slot, pl.ds(slices + s, 1), :] = jnp.sum(imag, axis=0, keepdims=True)
        xsend[slot, pl.ds(2 * slices + s, 1), :] = jnp.broadcast_to(mine[s], (1, lanes))
    exchange(slot, n, me, x_copy, xsend, xrecv)
    x_wait(slot)
    all_peaks = [xrecv[slot, d, pl.ds(2 * slices, slices), :] for d in range(n)]
    top_peak = functools.reduce(jnp.maximum, all_peaks)
    inverse = 1.0 / top_peak
    real = jnp.zeros((slices, lanes), jnp.float32)
    imag = jnp.zeros((slices, lanes), jnp.float32)
    for d in range(n):
        ratio = all_peaks[d] * inverse
        real = real + xrecv[slot, d, pl.ds(0, slices), :] * ratio
        imag = imag + xrecv[slot, d, pl.ds(slices, slices), :] * ratio
    real = jnp.sum(real, axis=1, keepdims=True) * factor
    imag = jnp.sum(imag, axis=1, keepdims=True) * factor
    log = jnp.log(top_peak)[:, :1] + jnp.concatenate(logs, axis=0)
    amp_ref[...] = jnp.concatenate([real, imag], axis=1)
    log_ref[...] = log
    top = jnp.max(log, axis=0, keepdims=True)
    share = jnp.exp(log - top)
    zsend[pl.ds(0, 1), :] = jnp.broadcast_to(jnp.sum(real * share, axis=0, keepdims=True), (1, lanes))
    zsend[pl.ds(1, 1), :] = jnp.broadcast_to(jnp.sum(imag * share, axis=0, keepdims=True), (1, lanes))
    zsend[pl.ds(2, 1), :] = jnp.broadcast_to(top, (1, lanes))
    zrecv[mz] = zsend[...]
    for k in range(1, nz):
        z_copy(lax.rem(mz + k, nz)).start()
    for k in range(1, nz):
        source = lax.rem(mz + k, nz)
        pltpu.make_async_remote_copy(
            src_ref=zsend,
            dst_ref=zrecv.at[source],
            send_sem=z_send.at[source],
            recv_sem=z_recv.at[source],
            device_id=(me, source),
            device_id_type=MESH,
        ).wait_recv()
    tops = [zrecv[z, pl.ds(2, 1), :] for z in range(nz)]
    top = functools.reduce(jnp.maximum, tops)
    real = jnp.zeros((1, lanes), jnp.float32)
    imag = jnp.zeros((1, lanes), jnp.float32)
    for z in range(nz):
        share = jnp.exp(tops[z] - top)
        real = real + zrecv[z, pl.ds(0, 1), :] * share
        imag = imag + zrecv[z, pl.ds(1, 1), :] * share
    total_ref[...] = jnp.concatenate([real[:, :1], imag[:, :1]], axis=1)
    top_ref[...] = top[:, :1]

    for k in range(1, nz):
        z_copy(lax.rem(mz + k, nz)).wait_send()
    for cl in range(per_col):
        for part in range(3):
            for k in range(1, n):
                gate_copy(cl, part, lax.rem(me + k, n)).wait_send()
    if columns > 1:
        @pl.when(me > 0)
        def _():
            for column in range(columns - 1):
                halo_copy(column).wait_send()


def body(layout, assign, edge, gate_left, gate_right, phase_angle, close):
    n, nz = lax.axis_size("col"), lax.axis_size("cuts")
    rows, width, lanes = edge.shape
    per_col = gate_left.shape[0]
    columns, own, slices = n * per_col, rows // n, assign.shape[0]
    rounds = -(-columns // SEGMENT)
    cosine, sine = jnp.cos(phase_angle), jnp.sin(phase_angle)
    cosine = jnp.concatenate([cosine, cosine], axis=1)
    sine = jnp.concatenate([sine, sine], axis=1)
    f32 = jnp.float32
    vmem = pl.BlockSpec(memory_space=pltpu.VMEM)
    smem = pl.BlockSpec(memory_space=pltpu.SMEM)
    dma = pltpu.SemaphoreType.DMA
    message = -(-3 * slices // 8) * 8
    phase_rows = -(-2 * slices // 8) * 8
    amp, log, total, top = pl.pallas_call(
        functools.partial(kernel, n, nz, rows),
        out_shape=[
            jax.ShapeDtypeStruct((slices, 2), f32),
            jax.ShapeDtypeStruct((slices, 1), f32),
            jax.ShapeDtypeStruct((1, 2), f32),
            jax.ShapeDtypeStruct((1, 1), f32),
        ],
        in_specs=[smem, smem] + [vmem] * 6,
        out_specs=[vmem] * 4,
        scratch_shapes=[
            pltpu.VMEM((per_col, 2, rows, width, lanes), f32),
            pltpu.VMEM((per_col, phase_rows, lanes), f32),
            pltpu.VMEM((columns, 2, own, width, lanes), f32),
            pltpu.VMEM((columns, phase_rows, lanes), f32),
            pltpu.VMEM((columns, own, slices, width, lanes), f32),
            pltpu.VMEM((columns, slices, width, lanes), f32),
            pltpu.VMEM((slices, 8, lanes), f32),
            pltpu.VMEM((rounds, message, lanes), f32),
            pltpu.VMEM((rounds, n, message, lanes), f32),
            pltpu.VMEM((8, lanes), f32),
            pltpu.VMEM((nz, 8, lanes), f32),
            dma((per_col, 3, n)),
            dma((columns, 3)),
            dma((columns,)),
            dma((columns,)),
            dma((rounds, n)),
            dma((rounds, n)),
            dma((nz,)),
            dma((nz,)),
        ],
        compiler_params=pltpu.CompilerParams(
            collective_id=0, has_side_effects=True, vmem_limit_bytes=48 * 1024 * 1024
        ),
    )(layout, assign, edge, gate_left, gate_right, cosine, sine, close)
    return amp, log.reshape(slices), total.reshape(2), top.reshape(())


def solution(mesh):
    in_specs = (
        P(None, "col"),
        P("cuts", "col"),
        P(),
        P("col", None, None, None),
        P("col", None, None, None),
        P(),
        P(),
    )
    out_specs = (P("cuts", None), P("cuts"), P(), P())
    return jax.shard_map(body, mesh=mesh, in_specs=in_specs, out_specs=out_specs, check_vma=False)
```

time: 235 us -> 51.8 us (0.22)
  starting transfers between devices: 95.8 us -> 0 us
  blocking collectives: 57.6 us -> 0 us
  Pallas kernels: 0 us -> 41.7 us
  other arithmetic: 20.2 us -> 0.7 us
  loops' own time: 19.3 us -> 0 us
  local copies, waits for them, and re-layouts: 23.5 us -> 6.58 us
  matrix products: 16.6 us -> 0 us
    ppermute x11 -> x0, starting transfers between devices: 95.8 us -> none  [from_behind(): return lax.ppermute(value, axis, pairs)]
    psum x2 -> x0, blocking collectives: 43.5 us -> none  [the longest x1 34.6 us: body(): amps, logs = lax.psum((amps, logs), 'col')]
    pallas_call x0 -> x1, Pallas kernels: none -> 41.7 us  [body(): pl.pallas_call(functools.partial(kernel, n, nz, rows), out_shape=[jax.Sha...]
    another operation x12 -> x0, loops' own time: 19.3 us -> none  [the longest x1 14 us: body(): lax.fori_loop(0, sections + groups - 1, section, initial)]
    dot_general x22 -> x0, matrix products: 16.6 us -> none  [the longest x4 4.18 us: sweep_column(): jnp.einsum('rpka,srab->srkpb', left_four, mixed, precision=lax.Precision....]
    pmax x1 -> x0, blocking collectives: 14 us -> none  [body(): top_log = lax.pmax(local_top, 'cuts')]
    reduce_sum x12 -> x0, other arithmetic: 10.8 us -> none  [the longest x11 10.7 us: amplitude(): jnp.sum(b_real * c_real - b_imag * c_imag, axis=(1, 2, 3)) * factor]
    while x46 -> x0, local copies, waits for them, and re-layouts: 9.1 us -> none
  transfers between devices with their start and end apart: 11 -> 0, of which waited for: 0 -> 0; matrix products, arithmetic and copies ran while one was open for 6% -> 0% of each run, Pallas kernels for 0% -> 0%
where the time goes in v1:
time: 51.8 us; the launch traced here: 51.5 us
  Pallas kernels  41.7 us (81%)
  local copies, waits for them, and re-layouts  6.58 us (13%)
  between operations  2.48 us (5%)
  other arithmetic  0.7 us (1%)
    pallas_call x1, Pallas kernels, body(): pl.pallas_call(functools.partial(kernel, n, nz, rows), out_shape=[jax.Sha...  41.7 us
    unnamed x16, local copies, waits for them, and re-layouts  6.54 us

profile of v1, /device:TPU:0, one launch (start us, length us, event | category | flops | bytes accessed | tf_op | source)
XLA Modules:
  0.0 51.5 jit_solution(122261058298250418)
XLA Ops:
  0.6 0.0 copy-start.4
  0.6 0.7 %copy.15.assign_ref = s32[4,1]{1,0:T(4,128)S(1)} copy(s32[4,1]{0,1:T(1,128)} %param.8) | data formatting | bytes 32 | tf_op args[1]
  1.4 0.0 copy-done.4
  1.4 0.1 pad_maximum_fusion
  1.5 0.0 copy-start.5
  1.5 0.7 %copy-done.5 = s32[16,1]{0,1:T(1,128)S(1)} copy-done((s32[16,1]{0,1:T(1,128)S(1)}, s32[16,1]{0,1:T(1,128)}, u32[]{:S(2)}) %copy-start.5) | copy-done | bytes 88
  2.2 0.1 copy.14.layout_ref
  2.3 0.0 copy-start
  2.3 1.0 %copy-done = f32[16,64,128]{2,1,0:T(8,128)S(1)} copy-done((f32[16,64,128]{2,1,0:T(8,128)S(1)}, f32[16,64,128]{2,1,0:T(8,128)}, u32[]{:S(2)}) %copy-start) | copy-done | bytes 524312
  3.3 0.0 copy-start.1
  3.3 0.9 %copy-done.1 = bf16[16,64,128]{2,1,0:T(8,128)(2,1)S(1)} copy-done((bf16[16,64,128]{2,1,0:T(8,128)(2,1)S(1)}, bf16[16,64,128]{2,1,0:T(8,128)(2,1)}, u32[]{:S(2)}) %copy-start.1) | copy-done | bytes 262168
  4.2 0.0 copy-start.2
  4.2 0.9 %copy-done.2 = bf16[1,16,64,128]{3,2,1,0:T(8,128)(2,1)S(1)} copy-done((bf16[1,16,64,128]{3,2,1,0:T(8,128)(2,1)S(1)}, bf16[1,16,64,128]{3,2,1,0:T(8,128)(2,1)}, u32[]{:S(2)}) %copy-start.2) | copy-done | bytes 262168
  5.2 0.0 copy-start.3
  5.2 0.9 %copy-done.3 = bf16[1,16,64,128]{3,2,1,0:T(8,128)(2,1)S(1)} copy-done((bf16[1,16,64,128]{3,2,1,0:T(8,128)(2,1)S(1)}, bf16[1,16,64,128]{3,2,1,0:T(8,128)(2,1)}, u32[]{:S(2)}) %copy-start.3) | copy-done | bytes 262168
  6.1 41.7 %shard_map.102 = (f32[4,2]{1,0:T(4,128)S(1)}, f32[4,1]{1,0:T(4,128)S(1)}, f32[1,2]{1,0:T(1,128)S(1)}, f32[1,1]{1,0:T(1,128)}) custom-call(s32[16,1]{1,0:T(8,128)S(1)} %copy.14.layout_ref, s32[4,1]{1,0:T(4,128)S(1)} %copy.15.assign_ref, bf16[16,64,128]{2,1,0:T(8,128)(2,1)S(1)} %copy-done.1, bf16[1,16,64,128]{3,2,1,0:T(8,128)(2,1)S(1)} %copy-done.2, ...), custom_call_target="tpu_custom_call" | custom-call | tf_op jit(solution)/shard_map/pallas_call | solution.py:364
  47.9 0.6 %copy.16 = f32[4,2]{0,1:T(2,128)} copy(f32[4,2]{1,0:T(4,128)S(1)} %get-tuple-element.16) | data formatting | bytes 64
  48.5 0.6 %reduce = f32[4]{0:T(128)} reduce(f32[4,1]{1,0:T(4,128)S(1)} %get-tuple-element.9, f32[]{:T(128)} %constant.4), dimensions={1}, to_apply=%get-tuple-element.9.reduce_sub_computation | reduce | bytes 36 | tf_op jit(solution)/shard_map/pallas_call | solution.py:364
  49.2 0.5 copy.19
  (1 shorter events, 0.0 us)
Async XLA Ops:
  0.6 0.8 %copy-start.4 = (f32[4,64]{1,0:T(4,128)S(1)}, f32[4,64]{1,0:T(4,128)}, u32[]{:S(2)}) copy-start(f32[4,64]{1,0:T(4,128)} %param.12) | copy-start | bytes 3076
  1.5 0.7 %copy-start.5 = (s32[16,1]{0,1:T(1,128)S(1)}, s32[16,1]{0,1:T(1,128)}, u32[]{:S(2)}) copy-start(s32[16,1]{0,1:T(1,128)} %param.7) | copy-start | bytes 196
  2.3 1.0 %copy-start = (f32[16,64,128]{2,1,0:T(8,128)S(1)}, f32[16,64,128]{2,1,0:T(8,128)}, u32[]{:S(2)}) copy-start(f32[16,64,128]{2,1,0:T(8,128)} %close_ref.1) | copy-start | bytes 1572868
  3.3 0.9 %copy-start.1 = (bf16[16,64,128]{2,1,0:T(8,128)(2,1)S(1)}, bf16[16,64,128]{2,1,0:T(8,128)(2,1)}, u32[]{:S(2)}) copy-start(bf16[16,64,128]{2,1,0:T(8,128)(2,1)} %edge_ref.1) | copy-start | bytes 786436
  4.2 0.9 %copy-start.2 = (bf16[1,16,64,128]{3,2,1,0:T(8,128)(2,1)S(1)}, bf16[1,16,64,128]{3,2,1,0:T(8,128)(2,1)}, u32[]{:S(2)}) copy-start(bf16[1,16,64,128]{3,2,1,0:T(8,128)(2,1)} %left_ref.1) | copy-start | bytes 786436
  5.2 0.9 %copy-start.3 = (bf16[1,16,64,128]{3,2,1,0:T(8,128)(2,1)S(1)}, bf16[1,16,64,128]{3,2,1,0:T(8,128)(2,1)}, u32[]{:S(2)}) copy-start(bf16[1,16,64,128]{3,2,1,0:T(8,128)(2,1)} %right_ref.1) | copy-start | bytes 786436

commit v2 on v1

--- a/solution.py
+++ b/solution.py
@@ -22,11 +22,21 @@
     return pltpu.roll(value, width, len(value.shape) - 1)
 
 
+def position(device, n):
+    if n % 8:
+        return device
+    chip = lax.rem(device // 2, 4)
+    return device + 2 * (chip // 2) * (1 - 2 * lax.rem(chip, 2))
+
+
+device_at = position
+
+
 def kernel(
     n, nz, rows,
-    layout_ref, assign_ref, edge_ref, left_ref, right_ref, cos_ref, sin_ref, close_ref,
+    layout_ref, assign_ref, edge_hbm, left_hbm, right_hbm, angle_ref, close_hbm,
     amp_ref, log_ref, total_ref, top_ref,
-    stage, stage_phase, gates, phases, board, halo, peak, xsend, xrecv, zsend, zrecv,
+    edge_ref, left_ref, right_ref, close_ref, cos_ref, sin_ref, load_sem, stage, stage_phase, gates, phases, board, halo, peak, xsend, xrecv, zsend, zrecv,
     gate_send, gate_recv, halo_send, halo_recv, x_send, x_recv, z_send, z_recv,
 ):
     me = lax.axis_index("col")
@@ -34,10 +44,27 @@
     per_col = left_ref.shape[0]
     columns = n * per_col
     own = rows // n
-    slices = assign_ref.shape[0]
+    slices = assign_ref.shape[1]
+    pieces = 2 if slices % 2 == 0 else 1
+    part_size = slices // pieces
     width = left_ref.shape[2]
     lanes = 2 * width
-    last = me == n - 1
+    place = position(me, n)
+    last = place == n - 1
+    next_row = jnp.minimum((place + 1) * own, rows - 1)
+    loads = [
+        pltpu.make_async_copy(left_hbm, left_ref, load_sem.at[0]),
+        pltpu.make_async_copy(right_hbm, right_ref, load_sem.at[1]),
+        pltpu.make_async_copy(
+            edge_hbm.at[pl.ds(place * own, own)], edge_ref.at[pl.ds(0, own)], load_sem.at[2]
+        ),
+        pltpu.make_async_copy(
+            edge_hbm.at[pl.ds(next_row, 1)], edge_ref.at[pl.ds(own, 1)], load_sem.at[3]
+        ),
+        pltpu.make_async_copy(close_hbm.at[pl.ds(place * own, own)], close_ref, load_sem.at[4]),
+    ]
+    for load in loads:
+        load.start()
 
     barrier = pltpu.get_barrier_semaphore()
     for k in range(1, n):
@@ -52,28 +79,35 @@
     lane = lax.broadcasted_iota(jnp.int32, (1, lanes), 1)
     sign = jnp.where(lane < width, -1.0, 1.0).astype(jnp.float32)
 
-    for cl in range(per_col):
-        for s in range(slices):
-            value = assign_ref[s, cl]
-            stage_phase[cl, pl.ds(s, 1), :] = cos_ref[pl.ds(value, 1), :]
-            stage_phase[cl, pl.ds(slices + s, 1), :] = sin_ref[pl.ds(value, 1), :] * sign
-        for r in range(rows):
-            kind = layout_ref[r, cl]
-            stage[cl, 0, r] = left_ref[cl, kind].astype(jnp.float32)
-            stage[cl, 1, r] = right_ref[cl, kind].astype(jnp.float32)
+    angle = angle_ref[...]
+    cosine, sine = jnp.cos(angle), jnp.sin(angle)
+    cos_ref[...] = jnp.concatenate([cosine, cosine], axis=1)
+    sin_ref[...] = jnp.concatenate([-sine, sine], axis=1)
     for s in range(slices):
         peak[s] = jnp.ones(peak.shape[1:], jnp.float32)
 
     @pl.when(last)
     def _():
         halo[...] = jnp.zeros_like(halo)
+
+    loads[0].wait()
+    loads[1].wait()
+    for cl in range(per_col):
+        for s in range(slices):
+            value = assign_ref[cl, s]
+            stage_phase[cl, pl.ds(s, 1), :] = cos_ref[pl.ds(value, 1), :]
+            stage_phase[cl, pl.ds(slices + s, 1), :] = sin_ref[pl.ds(value, 1), :]
+        for r in range(rows):
+            kind = layout_ref[cl, r]
+            stage[cl, 0, r] = left_ref[cl, kind].astype(jnp.float32)
+            stage[cl, 1, r] = right_ref[cl, kind].astype(jnp.float32)
 
     def gate_copy(cl, part, target):
         column = me * per_col + cl
         if part == 2:
             source, sink = stage_phase.at[cl], phases.at[column]
         else:
-            source = stage.at[cl, part, pl.ds(target * own, own)]
+            source = stage.at[cl, part, pl.ds(position(target, n) * own, own)]
             sink = gates.at[column, part]
         return pltpu.make_async_remote_copy(
             src_ref=source,
@@ -86,14 +120,15 @@
 
     pl.semaphore_wait(barrier, n - 1 + nz - 1)
     for cl in range(per_col):
-        for part in (2, 0, 1):
-            for k in range(1, n):
-                gate_copy(cl, part, lax.rem(me + k, n)).start()
+        for k in range(1, n):
+            target = device_at(lax.rem(place + n - k, n), n)
+            for part in (2, 0, 1):
+                gate_copy(cl, part, target).start()
     for cl in range(per_col):
         column = me * per_col + cl
         phases[column] = stage_phase[cl]
         for part in range(2):
-            gates[column, part] = stage[cl, part, pl.ds(me * own, own)]
+            gates[column, part] = stage[cl, part, pl.ds(place * own, own)]
 
     def wait_gates(column, part):
         sink = phases.at[column] if part == 2 else gates.at[column, part]
@@ -109,17 +144,18 @@
                 device_id_type=MESH,
             ).wait_recv()
 
-    def halo_copy(column):
+    def halo_copy(column, piece):
+        part = pl.ds(piece * part_size, part_size)
         return pltpu.make_async_remote_copy(
-            src_ref=board.at[column, 0],
-            dst_ref=halo.at[column],
-            send_sem=halo_send.at[column],
-            recv_sem=halo_recv.at[column],
-            device_id=(lax.rem(me + n - 1, n), mz),
+            src_ref=board.at[column, 0, part],
+            dst_ref=halo.at[column, part],
+            send_sem=halo_send.at[column, piece],
+            recv_sem=halo_recv.at[column, piece],
+            device_id=(device_at(lax.rem(place + n - 1, n), n), mz),
             device_id_type=MESH,
         )
 
-    def one_row(column, r, mixed, right_wait):
+    def one_row(column, r, mixed, right_wait, send):
         left = gates[column, 0, r].astype(jnp.bfloat16)
         left = jnp.concatenate([left, left], axis=1)
         stacks = []
@@ -156,41 +192,33 @@
             board[column, r, s] = turned
             size = jnp.abs(turned).reshape(width // 8, 8, lanes)
             peak[s] = jnp.maximum(peak[s], jnp.max(size, axis=0))
-
-    def after_row(column, r):
-        if r == 0:
-            @pl.when(me > 0)
-            def _():
-                halo_copy(column).start()
-
+            if send and (s + 1) % part_size == 0:
+                @pl.when(place > 0)
+                def _():
+                    halo_copy(column, s // part_size).start()
+
+    for load in loads[2:]:
+        load.wait()
     wait_gates(0, 0)
     for r in range(own):
-        row = me * own + r
-        here = edge_ref[row].astype(jnp.float32)
-        if r + 1 < own:
-            below = 0.5 * edge_ref[row + 1].astype(jnp.float32)
-        else:
-            weight = jnp.where(last, 0.0, 0.5).astype(jnp.float32)
-            below = weight * edge_ref[jnp.minimum(row + 1, rows - 1)].astype(jnp.float32)
-        one_row(0, r, [here + below], r == 0)
-        if columns > 1:
-            after_row(0, r)
+        below = edge_ref[r + 1].astype(jnp.float32)
+        weight = 0.5 if r + 1 < own else jnp.where(last, 0.0, 0.5).astype(jnp.float32)
+        mixed = edge_ref[r].astype(jnp.float32) + weight * below
+        one_row(0, r, [mixed], r == 0, r == 0 and columns > 1)
 
     def column_step(column, scale, send):
         wait_gates(column, 0)
         for r in range(own):
-            if r + 1 == own:
-                @pl.when(jnp.logical_not(last))
-                def _():
-                    halo_copy(column - 1).wait_recv()
             mixed = []
             for s in range(slices):
+                if r + 1 == own and s % part_size == 0:
+                    @pl.when(jnp.logical_not(last))
+                    def _():
+                        halo_copy(column - 1, s // part_size).wait_recv()
                 below = board[column - 1, r + 1, s] if r + 1 < own else halo[column - 1, s]
                 m = board[column - 1, r, s] + 0.5 * below
                 mixed.append(m if scale is None else m * scale[s])
-            one_row(column, r, mixed, r == 0)
-            if send:
-                after_row(column, r)
+            one_row(column, r, mixed, r == 0, send and r == 0)
 
     def exchange(slot, count, index, axis_copy, sender, receiver):
         def copy(target):
@@ -281,7 +309,7 @@
         imag = jnp.zeros((8, lanes), jnp.float32)
         inverse = 1.0 / mine[s]
         for r in range(own):
-            close = close_ref[me * own + r]
+            close = close_ref[r]
             value = board[columns - 1, r, s] * inverse
             real = real + jnp.sum((value * close).reshape(width // 8, 8, lanes), axis=0)
             imag = imag + jnp.sum((value * swap(close, width)).reshape(width // 8, 8, lanes), axis=0)
@@ -302,8 +330,9 @@
     real = jnp.sum(real, axis=1, keepdims=True) * factor
     imag = jnp.sum(imag, axis=1, keepdims=True) * factor
     log = jnp.log(top_peak)[:, :1] + jnp.concatenate(logs, axis=0)
-    amp_ref[...] = jnp.concatenate([real, imag], axis=1)
-    log_ref[...] = log
+    for s in range(slices):
+        amp_ref[:, pl.ds(s, 1)] = jnp.concatenate([real[s:s + 1], imag[s:s + 1]], axis=0)
+        log_ref[:, pl.ds(s, 1)] = log[s:s + 1]
     top = jnp.max(log, axis=0, keepdims=True)
     share = jnp.exp(log - top)
     zsend[pl.ds(0, 1), :] = jnp.broadcast_to(jnp.sum(real * share, axis=0, keepdims=True), (1, lanes))
@@ -340,10 +369,11 @@
             for k in range(1, n):
                 gate_copy(cl, part, lax.rem(me + k, n)).wait_send()
     if columns > 1:
-        @pl.when(me > 0)
+        @pl.when(place > 0)
         def _():
             for column in range(columns - 1):
-                halo_copy(column).wait_send()
+                for piece in range(pieces):
+                    halo_copy(column, piece).wait_send()
 
 
 def body(layout, assign, edge, gate_left, gate_right, phase_angle, close):
@@ -352,11 +382,10 @@
     per_col = gate_left.shape[0]
     columns, own, slices = n * per_col, rows // n, assign.shape[0]
     rounds = -(-columns // SEGMENT)
-    cosine, sine = jnp.cos(phase_angle), jnp.sin(phase_angle)
-    cosine = jnp.concatenate([cosine, cosine], axis=1)
-    sine = jnp.concatenate([sine, sine], axis=1)
+    pieces = 2 if slices % 2 == 0 else 1
     f32 = jnp.float32
     vmem = pl.BlockSpec(memory_space=pltpu.VMEM)
+    hbm = pl.BlockSpec(memory_space=pltpu.HBM)
     smem = pl.BlockSpec(memory_space=pltpu.SMEM)
     dma = pltpu.SemaphoreType.DMA
     message = -(-3 * slices // 8) * 8
@@ -364,14 +393,21 @@
     amp, log, total, top = pl.pallas_call(
         functools.partial(kernel, n, nz, rows),
         out_shape=[
-            jax.ShapeDtypeStruct((slices, 2), f32),
-            jax.ShapeDtypeStruct((slices, 1), f32),
+            jax.ShapeDtypeStruct((2, slices), f32),
+            jax.ShapeDtypeStruct((1, slices), f32),
             jax.ShapeDtypeStruct((1, 2), f32),
             jax.ShapeDtypeStruct((1, 1), f32),
         ],
-        in_specs=[smem, smem] + [vmem] * 6,
+        in_specs=[smem, smem, hbm, hbm, hbm, vmem, hbm],
         out_specs=[vmem] * 4,
         scratch_shapes=[
+            pltpu.VMEM((own + 1, width, lanes), edge.dtype),
+            pltpu.VMEM(gate_left.shape, gate_left.dtype),
+            pltpu.VMEM(gate_right.shape, gate_right.dtype),
+            pltpu.VMEM((own, width, lanes), f32),
+            pltpu.VMEM((phase_angle.shape[0], lanes), f32),
+            pltpu.VMEM((phase_angle.shape[0], lanes), f32),
+            dma((5,)),
             pltpu.VMEM((per_col, 2, rows, width, lanes), f32),
             pltpu.VMEM((per_col, phase_rows, lanes), f32),
             pltpu.VMEM((columns, 2, own, width, lanes), f32),
@@ -385,18 +421,18 @@
             pltpu.VMEM((nz, 8, lanes), f32),
             dma((per_col, 3, n)),
             dma((columns, 3)),
-            dma((columns,)),
-            dma((columns,)),
+            dma((columns, pieces)),
+            dma((columns, pieces)),
             dma((rounds, n)),
             dma((rounds, n)),
             dma((nz,)),
             dma((nz,)),
         ],
         compiler_params=pltpu.CompilerParams(
-            collective_id=0, has_side_effects=True, vmem_limit_bytes=48 * 1024 * 1024
+            collective_id=0, has_side_effects=True, vmem_limit_bytes=67_000_000
         ),
-    )(layout, assign, edge, gate_left, gate_right, cosine, sine, close)
-    return amp, log.reshape(slices), total.reshape(2), top.reshape(())
+    )(layout.T, assign.T, edge, gate_left, gate_right, phase_angle, close)
+    return amp.T, log.reshape(slices), total.reshape(2), top.reshape(())
 
 
 def solution(mesh):

time: 51.8 us -> 44.5 us (0.86)
  local copies, waits for them, and re-layouts: 6.58 us -> 2.34 us
  Pallas kernels: 41.7 us -> 39.5 us
  other arithmetic: 0.7 us -> 0 us
    unnamed x16 -> x9, local copies, waits for them, and re-layouts: 6.54 us -> 2.34 us
    pallas_call x1, Pallas kernels: 41.7 us -> 39.5 us  [body(): pl.pallas_call(functools.partial(kernel, n, nz, rows), out_shape=[jax.Sha...]
    pallas_call x1 -> x0, other arithmetic: 0.63 us -> none  [body(): pl.pallas_call(functools.partial(kernel, n, nz, rows), out_shape=[jax.Sha...]
where the time goes in v2:
time: 44.5 us; the launch traced here: 44.3 us
  Pallas kernels  39.5 us (89%)
  between operations  2.47 us (6%)
  local copies, waits for them, and re-layouts  2.34 us (5%)
    pallas_call x1, Pallas kernels, body(): pl.pallas_call(functools.partial(kernel, n, nz, rows), out_shape=[jax.Sha...  39.5 us
    unnamed x9, local copies, waits for them, and re-layouts  2.34 us

profile of v2, /device:TPU:0, one launch (start us, length us, event | category | flops | bytes accessed | tf_op | source)
XLA Modules:
  0.0 44.3 jit_solution(4296052085667184798)
XLA Ops:
  0.6 39.5 %shard_map.102 = (f32[2,4]{1,0:T(2,128)}, f32[1,4]{1,0:T(1,128)}, f32[1,2]{1,0:T(1,128)}, f32[1,1]{1,0:T(1,128)}) custom-call(s32[1,16]{1,0:T(1,128)} %bitcast.7, s32[1,4]{1,0:T(1,128)} %bitcast.8, bf16[16,64,128]{2,1,0:T(8,128)(2,1)} %edge_hbm.1, bf16[1,16,64,128]{3,2,1,0:T(8,128)(2,1)} %left_hbm.1, bf16[1,16,64,128]{3,2,1,0:T(8,128)(2,1)} %right_hbm.1, ...), custom_call_target="tpu_custom_call" | custom-call | tf_op jit(solution)/shard_map/pallas_call | solution.py:393
  40.1 0.0 copy-start
  40.1 0.6 %copy-done = f32[2,4]{1,0:T(2,128)S(1)} copy-done((f32[2,4]{1,0:T(2,128)S(1)}, f32[2,4]{1,0:T(2,128)}, u32[]{:S(2)}) %copy-start) | copy-done | bytes 56
  40.7 0.0 copy-start.2
  40.8 0.6 %copy.15 = f32[4,2]{0,1:T(2,128)} copy(f32[4,2]{0,1:T(2,128)S(1)} %bitcast.6) | data formatting | bytes 64
  41.3 0.0 copy-done.2
  41.4 0.0 copy-start.1
  41.4 0.5 %copy.16 = f32[4]{0:T(128)} copy(f32[4]{0:T(128)S(1)} %bitcast.10) | data formatting | bytes 32
  41.9 0.1 copy-done.1
  42.0 0.5 %copy.17 = f32[2]{0:T(128)} copy(f32[2]{0:T(128)S(1)} %bitcast.9) | data formatting | bytes 16
Async XLA Ops:
  40.1 0.6 %copy-start = (f32[2,4]{1,0:T(2,128)S(1)}, f32[2,4]{1,0:T(2,128)}, u32[]{:S(2)}) copy-start(f32[2,4]{1,0:T(2,128)} %get-tuple-element.8) | copy-start | bytes 100
  40.7 0.6 %copy-start.2 = (f32[1,4]{1,0:T(1,128)S(1)}, f32[1,4]{1,0:T(1,128)}, u32[]{:S(2)}) copy-start(f32[1,4]{1,0:T(1,128)} %get-tuple-element.9) | copy-start | bytes 52
  41.4 0.6 %copy-start.1 = (f32[1,2]{1,0:T(1,128)S(1)}, f32[1,2]{1,0:T(1,128)}, u32[]{:S(2)}) copy-start(f32[1,2]{1,0:T(1,128)} %get-tuple-element.10) | copy-start | bytes 28

commit v3 on v2

--- a/solution.py
+++ b/solution.py
@@ -35,9 +35,9 @@
 def kernel(
     n, nz, rows,
     layout_ref, assign_ref, edge_hbm, left_hbm, right_hbm, angle_ref, close_hbm,
-    amp_ref, log_ref, total_ref, top_ref,
+    result_ref,
     edge_ref, left_ref, right_ref, close_ref, cos_ref, sin_ref, load_sem, stage, stage_phase, gates, phases, board, halo, peak, xsend, xrecv, zsend, zrecv,
-    gate_send, gate_recv, halo_send, halo_recv, x_send, x_recv, z_send, z_recv,
+    gate_send, gate_recv, pass_send, halo_send, halo_recv, x_send, x_recv, z_send, z_recv,
 ):
     me = lax.axis_index("col")
     mz = lax.axis_index("cuts")
@@ -102,6 +102,20 @@
             stage[cl, 0, r] = left_ref[cl, kind].astype(jnp.float32)
             stage[cl, 1, r] = right_ref[cl, kind].astype(jnp.float32)
 
+    partner = mz + 1 - 2 * lax.rem(mz, 2) if nz % 2 == 0 else mz
+
+    def direct(column, target):
+        if nz % 2:
+            return target >= 0
+        near = (column // per_col) // 2 == target // 2
+        return jnp.logical_or(near, lax.rem(column, 2) == lax.rem(mz, 2))
+
+    def passes(column):
+        if nz % 2:
+            return me < 0
+        far = (column // per_col) // 2 != me // 2
+        return jnp.logical_and(far, lax.rem(column, 2) == lax.rem(mz, 2))
+
     def gate_copy(cl, part, target):
         column = me * per_col + cl
         if part == 2:
@@ -122,18 +136,42 @@
     for cl in range(per_col):
         for k in range(1, n):
             target = device_at(lax.rem(place + n - k, n), n)
-            for part in (2, 0, 1):
-                gate_copy(cl, part, target).start()
+            gate_copy(cl, 2, target).start()
+
+            @pl.when(direct(me * per_col + cl, target))
+            def _():
+                gate_copy(cl, 0, target).start()
+                gate_copy(cl, 1, target).start()
     for cl in range(per_col):
         column = me * per_col + cl
         phases[column] = stage_phase[cl]
         for part in range(2):
             gates[column, part] = stage[cl, part, pl.ds(place * own, own)]
 
+    def pass_copy(column, part):
+        return pltpu.make_async_remote_copy(
+            src_ref=gates.at[column, part],
+            dst_ref=gates.at[column, part],
+            send_sem=pass_send.at[column, part],
+            recv_sem=gate_recv.at[column, part],
+            device_id=(me, partner),
+            device_id_type=MESH,
+        )
+
+    def pass_on(column):
+        @pl.when(passes(column))
+        def _():
+            for part in range(2):
+                pass_copy(column, part).wait_recv()
+                pass_copy(column, part).start()
+
     def wait_gates(column, part):
         sink = phases.at[column] if part == 2 else gates.at[column, part]
-
-        @pl.when(column // per_col != me)
+        needed = column // per_col != me
+        if part < 2:
+            needed = jnp.logical_and(needed, jnp.logical_not(passes(column)))
+
+        @pl.when(needed)
         def _():
             pltpu.make_async_remote_copy(
                 src_ref=sink,
@@ -199,7 +237,11 @@
 
     for load in loads[2:]:
         load.wait()
+    for column in range(min(2, columns)):
+        pass_on(column)
     wait_gates(0, 0)
+    if columns > 2:
+        pass_on(2)
     for r in range(own):
         below = edge_ref[r + 1].astype(jnp.float32)
         weight = 0.5 if r + 1 < own else jnp.where(last, 0.0, 0.5).astype(jnp.float32)
@@ -208,6 +250,10 @@
 
     def column_step(column, scale, send):
         wait_gates(column, 0)
+
+        @pl.when(column + 2 < columns)
+        def _():
+            pass_on(jnp.minimum(column + 2, columns - 1))
         for r in range(own):
             mixed = []
             for s in range(slices):
@@ -330,9 +376,7 @@
     real = jnp.sum(real, axis=1, keepdims=True) * factor
     imag = jnp.sum(imag, axis=1, keepdims=True) * factor
     log = jnp.log(top_peak)[:, :1] + jnp.concatenate(logs, axis=0)
-    for s in range(slices):
-        amp_ref[:, pl.ds(s, 1)] = jnp.concatenate([real[s:s + 1], imag[s:s + 1]], axis=0)
-        log_ref[:, pl.ds(s, 1)] = log[s:s + 1]
+    result_ref[pl.ds(0, slices), :] = jnp.where(lane == 0, real, jnp.where(lane == 1, imag, log))
     top = jnp.max(log, axis=0, keepdims=True)
     share = jnp.exp(log - top)
     zsend[pl.ds(0, 1), :] = jnp.broadcast_to(jnp.sum(real * share, axis=0, keepdims=True), (1, lanes))
@@ -359,21 +403,40 @@
         share = jnp.exp(tops[z] - top)
         real = real + zrecv[z, pl.ds(0, 1), :] * share
         imag = imag + zrecv[z, pl.ds(1, 1), :] * share
-    total_ref[...] = jnp.concatenate([real[:, :1], imag[:, :1]], axis=1)
-    top_ref[...] = top[:, :1]
+    result_ref[pl.ds(slices, 1), :] = jnp.where(lane == 0, real, jnp.where(lane == 1, imag, top))
 
     for k in range(1, nz):
         z_copy(lax.rem(mz + k, nz)).wait_send()
     for cl in range(per_col):
-        for part in range(3):
-            for k in range(1, n):
-                gate_copy(cl, part, lax.rem(me + k, n)).wait_send()
+        for k in range(1, n):
+            target = lax.rem(me + k, n)
+            gate_copy(cl, 2, target).wait_send()
+
+            @pl.when(direct(me * per_col + cl, target))
+            def _():
+                gate_copy(cl, 0, target).wait_send()
+                gate_copy(cl, 1, target).wait_send()
+    for column in range(columns):
+        @pl.when(passes(column))
+        def _():
+            pass_copy(column, 0).wait_send()
+            pass_copy(column, 1).wait_send()
     if columns > 1:
         @pl.when(place > 0)
         def _():
             for column in range(columns - 1):
                 for piece in range(pieces):
                     halo_copy(column, piece).wait_send()
+
+
+def unpack(result_ref, amp_ref, log_ref, total_ref, top_ref):
+    slices = amp_ref.shape[1]
+    for s in range(slices):
+        for k in range(2):
+            amp_ref[pl.ds(k, 1), pl.ds(s, 1)] = result_ref[pl.ds(s, 1), pl.ds(k, 1)]
+        log_ref[:, pl.ds(s, 1)] = result_ref[pl.ds(s, 1), pl.ds(2, 1)]
+    total_ref[...] = result_ref[pl.ds(slices, 1), pl.ds(0, 2)]
+    top_ref[...] = result_ref[pl.ds(slices, 1), pl.ds(2, 1)]
 
 
 def body(layout, assign, edge, gate_left, gate_right, phase_angle, close):
@@ -390,16 +453,11 @@
     dma = pltpu.SemaphoreType.DMA
     message = -(-3 * slices // 8) * 8
     phase_rows = -(-2 * slices // 8) * 8
-    amp, log, total, top = pl.pallas_call(
+    result = pl.pallas_call(
         functools.partial(kernel, n, nz, rows),
-        out_shape=[
-            jax.ShapeDtypeStruct((2, slices), f32),
-            jax.ShapeDtypeStruct((1, slices), f32),
-            jax.ShapeDtypeStruct((1, 2), f32),
-            jax.ShapeDtypeStruct((1, 1), f32),
-        ],
+        out_shape=jax.ShapeDtypeStruct((-(-(slices + 1) // 8) * 8, lanes), f32),
         in_specs=[smem, smem, hbm, hbm, hbm, vmem, hbm],
-        out_specs=[vmem] * 4,
+        out_specs=vmem,
         scratch_shapes=[
             pltpu.VMEM((own + 1, width, lanes), edge.dtype),
             pltpu.VMEM(gate_left.shape, gate_left.dtype),
@@ -421,6 +479,7 @@
             pltpu.VMEM((nz, 8, lanes), f32),
             dma((per_col, 3, n)),
             dma((columns, 3)),
+            dma((columns, 2)),
             dma((columns, pieces)),
             dma((columns, pieces)),
             dma((rounds, n)),
@@ -432,6 +491,17 @@
             collective_id=0, has_side_effects=True, vmem_limit_bytes=67_000_000
         ),
     )(layout.T, assign.T, edge, gate_left, gate_right, phase_angle, close)
+    amp, log, total, top = pl.pallas_call(
+        unpack,
+        out_shape=[
+            jax.ShapeDtypeStruct((2, slices), f32),
+            jax.ShapeDtypeStruct((1, slices), f32),
+            jax.ShapeDtypeStruct((1, 2), f32),
+            jax.ShapeDtypeStruct((1, 1), f32),
+        ],
+        in_specs=[vmem],
+        out_specs=[vmem] * 4,
+    )(result)
     return amp.T, log.reshape(slices), total.reshape(2), top.reshape(())
 
 

time: 44.5 us -> 40.5 us (0.910)
  local copies, waits for them, and re-layouts: 2.34 us -> 0 us
  between operations: 2.47 us -> 0.64 us
    unnamed x9 -> x0, local copies, waits for them, and re-layouts: 2.34 us -> none
    pallas_call x1 -> x2, Pallas kernels: 39.5 us -> 39.7 us  [the longest x1 38.4 us: body(): pl.pallas_call(functools.partial(kernel, n, nz, rows), out_shape=jax.Shap...]
where the time goes in v3:
time: 40.5 us; the launch traced here: 40.3 us
  Pallas kernels  39.7 us (98%)
  between operations  0.64 us (2%)
    pallas_call x1, Pallas kernels, body(): pl.pallas_call(functools.partial(kernel, n, nz, rows), out_shape=jax.Shap...  38.4 us
    pallas_call x1, Pallas kernels, body(): pl.pallas_call(unpack, out_shape=[jax.ShapeDtypeStruct((2, slices), f32),...  1.32 us

profile of v3, /device:TPU:0, one launch (start us, length us, event | category | flops | bytes accessed | tf_op | source)
XLA Modules:
  0.0 40.3 jit_solution(2400649931361151802)
XLA Ops:
  0.6 38.4 %shard_map.102.result_ref = f32[8,128]{1,0:T(8,128)} custom-call(s32[1,16]{1,0:T(1,128)} %bitcast.6, s32[1,4]{1,0:T(1,128)} %bitcast.7, bf16[16,64,128]{2,1,0:T(8,128)(2,1)} %edge_hbm.1, bf16[1,16,64,128]{3,2,1,0:T(8,128)(2,1)} %left_hbm.1, bf16[1,16,64,128]{3,2,1,0:T(8,128)(2,1)} %right_hbm.1, f32[4,64]{1,0:T(4,128)} %angle_ref.1, f32[16,64,128]{2,1,0:T(8,128)} %close_hbm.1), custom_call_target="tpu_custom_call" | custom-call | tf_op jit(solution)/shard_map/pallas_call | solution.py:456
  39.0 1.3 %shard_map.103 = (f32[2,4]{1,0:T(2,128)}, f32[1,4]{1,0:T(1,128)}, f32[1,2]{1,0:T(1,128)}, f32[1,1]{1,0:T(1,128)}) custom-call(f32[8,128]{1,0:T(8,128)} %shard_map.102.result_ref), custom_call_target="tpu_custom_call" | custom-call | tf_op jit(solution)/shard_map/pallas_call | solution.py:494

commit v4 on v3

--- a/solution.py
+++ b/solution.py
@@ -240,20 +240,17 @@
     for column in range(min(2, columns)):
         pass_on(column)
     wait_gates(0, 0)
-    if columns > 2:
-        pass_on(2)
     for r in range(own):
         below = edge_ref[r + 1].astype(jnp.float32)
         weight = 0.5 if r + 1 < own else jnp.where(last, 0.0, 0.5).astype(jnp.float32)
         mixed = edge_ref[r].astype(jnp.float32) + weight * below
         one_row(0, r, [mixed], r == 0, r == 0 and columns > 1)
+        if r == 0 and columns > 2:
+            pass_on(2)
 
     def column_step(column, scale, send):
-        wait_gates(column, 0)
-
-        @pl.when(column + 2 < columns)
-        def _():
-            pass_on(jnp.minimum(column + 2, columns - 1))
+        for part in range(3):
+            wait_gates(column, part)
         for r in range(own):
             mixed = []
             for s in range(slices):
@@ -264,7 +261,11 @@
                 below = board[column - 1, r + 1, s] if r + 1 < own else halo[column - 1, s]
                 m = board[column - 1, r, s] + 0.5 * below
                 mixed.append(m if scale is None else m * scale[s])
-            one_row(column, r, mixed, r == 0, send and r == 0)
+            one_row(column, r, mixed, False, send and r == 0)
+            if r == 0:
+                @pl.when(column + 2 < columns)
+                def _():
+                    pass_on(jnp.minimum(column + 2, columns - 1))
 
     def exchange(slot, count, index, axis_copy, sender, receiver):
         def copy(target):

time: 40.5 us -> 41 us (1.012)
    pallas_call x1, Pallas kernels: 38.4 us -> 38.8 us  [body(): pl.pallas_call(functools.partial(kernel, n, nz, rows), out_shape=jax.Shap...]
where the time goes in v4:
time: 41 us; the launch traced here: 40.8 us
  Pallas kernels  40.1 us (98%)
  between operations  0.64 us (2%)
    pallas_call x1, Pallas kernels, body(): pl.pallas_call(functools.partial(kernel, n, nz, rows), out_shape=jax.Shap...  38.8 us
    pallas_call x1, Pallas kernels, body(): pl.pallas_call(unpack, out_shape=[jax.ShapeDtypeStruct((2, slices), f32),...  1.32 us

profile of v4, /device:TPU:0, one launch (start us, length us, event | category | flops | bytes accessed | tf_op | source)
XLA Modules:
  0.0 40.8 jit_solution(14921861597614026776)
XLA Ops:
  0.6 38.8 %shard_map.102.result_ref = f32[8,128]{1,0:T(8,128)} custom-call(s32[1,16]{1,0:T(1,128)} %bitcast.6, s32[1,4]{1,0:T(1,128)} %bitcast.7, bf16[16,64,128]{2,1,0:T(8,128)(2,1)} %edge_hbm.1, bf16[1,16,64,128]{3,2,1,0:T(8,128)(2,1)} %left_hbm.1, bf16[1,16,64,128]{3,2,1,0:T(8,128)(2,1)} %right_hbm.1, f32[4,64]{1,0:T(4,128)} %angle_ref.1, f32[16,64,128]{2,1,0:T(8,128)} %close_hbm.1), custom_call_target="tpu_custom_call" | custom-call | tf_op jit(solution)/shard_map/pallas_call | solution.py:457
  39.4 1.3 %shard_map.103 = (f32[2,4]{1,0:T(2,128)}, f32[1,4]{1,0:T(1,128)}, f32[1,2]{1,0:T(1,128)}, f32[1,1]{1,0:T(1,128)}) custom-call(f32[8,128]{1,0:T(8,128)} %shard_map.102.result_ref), custom_call_target="tpu_custom_call" | custom-call | tf_op jit(solution)/shard_map/pallas_call | solution.py:495

commit v5 on v4

--- a/solution.py
+++ b/solution.py
@@ -104,17 +104,17 @@
 
     partner = mz + 1 - 2 * lax.rem(mz, 2) if nz % 2 == 0 else mz
 
-    def direct(column, target):
+    def direct(column, target, part):
         if nz % 2:
             return target >= 0
         near = (column // per_col) // 2 == target // 2
-        return jnp.logical_or(near, lax.rem(column, 2) == lax.rem(mz, 2))
-
-    def passes(column):
+        return jnp.logical_or(near, part == lax.rem(mz, 2))
+
+    def passes(column, part):
         if nz % 2:
             return me < 0
         far = (column // per_col) // 2 != me // 2
-        return jnp.logical_and(far, lax.rem(column, 2) == lax.rem(mz, 2))
+        return jnp.logical_and(far, part == lax.rem(mz, 2))
 
     def gate_copy(cl, part, target):
         column = me * per_col + cl
@@ -138,10 +138,10 @@
             target = device_at(lax.rem(place + n - k, n), n)
             gate_copy(cl, 2, target).start()
 
-            @pl.when(direct(me * per_col + cl, target))
-            def _():
-                gate_copy(cl, 0, target).start()
-                gate_copy(cl, 1, target).start()
+            for part in range(2):
+                @pl.when(direct(me * per_col + cl, target, part))
+                def _():
+                    gate_copy(cl, part, target).start()
     for cl in range(per_col):
         column = me * per_col + cl
         phases[column] = stage_phase[cl]
@@ -159,9 +159,9 @@
         )
 
     def pass_on(column):
-        @pl.when(passes(column))
-        def _():
-            for part in range(2):
+        for part in range(2):
+            @pl.when(passes(column, part))
+            def _():
                 pass_copy(column, part).wait_recv()
                 pass_copy(column, part).start()
 
@@ -169,7 +169,7 @@
         sink = phases.at[column] if part == 2 else gates.at[column, part]
         needed = column // per_col != me
         if part < 2:
-            needed = jnp.logical_and(needed, jnp.logical_not(passes(column)))
+            needed = jnp.logical_and(needed, jnp.logical_not(passes(column, part)))
 
         @pl.when(needed)
         def _():
@@ -413,15 +413,15 @@
             target = lax.rem(me + k, n)
             gate_copy(cl, 2, target).wait_send()
 
-            @pl.when(direct(me * per_col + cl, target))
+            for part in range(2):
+                @pl.when(direct(me * per_col + cl, target, part))
+                def _():
+                    gate_copy(cl, part, target).wait_send()
+    for column in range(columns):
+        for part in range(2):
+            @pl.when(passes(column, part))
             def _():
-                gate_copy(cl, 0, target).wait_send()
-                gate_copy(cl, 1, target).wait_send()
-    for column in range(columns):
-        @pl.when(passes(column))
-        def _():
-            pass_copy(column, 0).wait_send()
-            pass_copy(column, 1).wait_send()
+                pass_copy(column, part).wait_send()
     if columns > 1:
         @pl.when(place > 0)
         def _():

time: 41 us -> 41 us (level)
  no operation moved by 1% of the time
where the time goes in v5:
time: 41 us; the launch traced here: 40.8 us
  Pallas kernels  40.2 us (98%)
  between operations  0.64 us (2%)
    pallas_call x1, Pallas kernels, body(): pl.pallas_call(functools.partial(kernel, n, nz, rows), out_shape=jax.Shap...  38.8 us
    pallas_call x1, Pallas kernels, body(): pl.pallas_call(unpack, out_shape=[jax.ShapeDtypeStruct((2, slices), f32),...  1.32 us

profile of v5, /device:TPU:0, one launch (start us, length us, event | category | flops | bytes accessed | tf_op | source)
XLA Modules:
  0.0 40.8 jit_solution(3909168768637099858)
XLA Ops:
  0.6 38.8 %shard_map.102.result_ref = f32[8,128]{1,0:T(8,128)} custom-call(s32[1,16]{1,0:T(1,128)} %bitcast.6, s32[1,4]{1,0:T(1,128)} %bitcast.7, bf16[16,64,128]{2,1,0:T(8,128)(2,1)} %edge_hbm.1, bf16[1,16,64,128]{3,2,1,0:T(8,128)(2,1)} %left_hbm.1, bf16[1,16,64,128]{3,2,1,0:T(8,128)(2,1)} %right_hbm.1, f32[4,64]{1,0:T(4,128)} %angle_ref.1, f32[16,64,128]{2,1,0:T(8,128)} %close_hbm.1), custom_call_target="tpu_custom_call" | custom-call | tf_op jit(solution)/shard_map/pallas_call | solution.py:457
  39.5 1.3 %shard_map.103 = (f32[2,4]{1,0:T(2,128)}, f32[1,4]{1,0:T(1,128)}, f32[1,2]{1,0:T(1,128)}, f32[1,1]{1,0:T(1,128)}) custom-call(f32[8,128]{1,0:T(8,128)} %shard_map.102.result_ref), custom_call_target="tpu_custom_call" | custom-call | tf_op jit(solution)/shard_map/pallas_call | solution.py:495
